TPU v7x, 32 devices: a 4x4x1 block of a 4x4x8 slice. The times are simulated.
32 devices in a mesh: data: 1 (over z), seq: 32 (over y, x, core).
Axes of the slice: x: 4, y: 4, z: 1, core: 2. Of those that a mesh axis runs over, the one named last changes fastest.
The devices are a block of a 4x4x8 slice.
Arguments:
- hidden: bfloat16 [3, 12288, 768], P('data', 'seq')
- positions: int32 [3, 12288], P('data', 'seq')
- g_attn: float32 [1, 768], replicated
- g_mlp: float32 [1, 768], replicated
- w_query: bfloat16 [1, 768, 12, 64], replicated
- w_key: bfloat16 [1, 768, 12, 64], replicated
- w_value: bfloat16 [1, 768, 12, 64], replicated
- w_out: bfloat16 [1, 768, 768], replicated
- w_gate: bfloat16 [1, 768, 3072], replicated
- w_up: bfloat16 [1, 768, 3072], replicated
- w_down: bfloat16 [1, 3072, 768], replicated
- d_out: bfloat16 [3, 12288, 768], P('data', 'seq')
Outputs:
- output 1: bfloat16 [3, 12288, 768], P('data', 'seq')
- output 2: float32 [1, 768], P(None, ('data', 'seq'))
- output 3: float32 [1, 768], P(None, ('data', 'seq'))
- output 4: float32 [1, 768, 12, 64], P(None, ('data', 'seq'))
- output 5: float32 [1, 768, 12, 64], P(None, ('data', 'seq'))
- output 6: float32 [1, 768, 12, 64], P(None, ('data', 'seq'))
- output 7: float32 [1, 768, 768], P(None, ('data', 'seq'))
- output 8: float32 [1, 768, 3072], P(None, ('data', 'seq'))
- output 9: float32 [1, 768, 3072], P(None, ('data', 'seq'))
- output 10: float32 [1, 3072, 768], P(None, ('data', 'seq'))
All inputs are finite; a program needn't handle non-finite values.
Results may differ from a plain program's by a relative error of at most 0.02.
Values are sent between devices in bfloat16 or wider.
A program may use at most 768 MiB of HBM per device.

v0:
```python
import functools
import math
import jax
import jax.numpy as jnp
from jax import lax
from jax.sharding import PartitionSpec as P

WINDOW = 256
NORM_EPS = 1e-5


def rope_tables(positions, head_dim):
    half_dim = head_dim // 2
    inv_freq = 1.0 / (10000.0 ** (jnp.arange(half_dim, dtype=jnp.float32) * (2.0 / head_dim)))
    angles = positions.astype(jnp.float32)[:, :, None] * inv_freq
    return jnp.cos(angles)[:, :, None, :], jnp.sin(angles)[:, :, None, :]


def rotate(values, cos_t, sin_t):
    half_dim = values.shape[-1] // 2
    first = values[..., :half_dim]
    second = values[..., half_dim:]
    return jnp.concatenate([first * cos_t - second * sin_t, second * cos_t + first * sin_t], axis=-1)


def rotate_back(grads, cos_t, sin_t):
    half_dim = grads.shape[-1] // 2
    first = grads[..., :half_dim]
    second = grads[..., half_dim:]
    return jnp.concatenate([first * cos_t + second * sin_t, second * cos_t - first * sin_t], axis=-1)


def rms_norm(hidden, gain_vec):
    hidden_f = hidden.astype(jnp.float32)
    inv_rms = lax.rsqrt(jnp.mean(hidden_f * hidden_f, axis=-1, keepdims=True) + NORM_EPS)
    unit_vals = hidden_f * inv_rms
    return (unit_vals * gain_vec).astype(jnp.bfloat16), unit_vals, inv_rms


def rms_norm_bwd(grad_normed, unit_vals, inv_rms, gain_vec):
    grad_unit = grad_normed * gain_vec
    grad_gain = jnp.sum(grad_normed * unit_vals, axis=(0, 1))
    grad_hidden = inv_rms * (grad_unit - unit_vals * jnp.mean(grad_unit * unit_vals, axis=-1, keepdims=True))
    return grad_hidden, grad_gain


def window_attention(q_rot, k_ext, v_ext, key_start):
    batch_rows, tok_local, kv_heads, q_group, head_dim = q_rot.shape
    qblock = math.gcd(tok_local, 128)
    span_len = qblock + WINDOW - 1
    row_ids = jnp.arange(qblock)[:, None]
    col_ids = jnp.arange(span_len)[None, :]
    band_mask = (col_ids >= row_ids) & (col_ids < row_ids + WINDOW)
    attn_scale = head_dim ** -0.5

    def one_block(blk_idx):
        blk_start = blk_idx * qblock
        q_blk = lax.dynamic_slice_in_dim(q_rot, blk_start, qblock, axis=1)
        k_blk = lax.dynamic_slice_in_dim(k_ext, blk_start, span_len, axis=1)
        v_blk = lax.dynamic_slice_in_dim(v_ext, blk_start, span_len, axis=1)
        scores = jnp.einsum('bqkgd,bckd->bkgqc', q_blk, k_blk, preferred_element_type=jnp.float32) * attn_scale
        keep_mask = band_mask & (blk_start + col_ids >= key_start)
        attn_probs = jax.nn.softmax(jnp.where(keep_mask, scores, -1e30), axis=-1).astype(jnp.bfloat16)
        out_blk = jnp.einsum('bkgqc,bckd->bqkgd', attn_probs, v_blk, preferred_element_type=jnp.float32)
        return out_blk.astype(jnp.bfloat16)

    blocks = lax.map(jax.checkpoint(one_block), jnp.arange(tok_local // qblock))
    return jnp.moveaxis(blocks, 0, 1).reshape(batch_rows, tok_local, kv_heads * q_group * head_dim)


def add_tail(own_grad, recv_grad):
    tail_start = own_grad.shape[1] - recv_grad.shape[1]
    head_part = own_grad[:, :tail_start].astype(jnp.float32)
    tail_part = own_grad[:, tail_start:].astype(jnp.float32) + recv_grad.astype(jnp.float32)
    return jnp.concatenate([head_part, tail_part], axis=1)


def solution(mesh):
    seq_size = mesh.shape['seq']
    to_right = [(src, src + 1) for src in range(seq_size - 1)]
    to_left = [(src + 1, src) for src in range(seq_size - 1)]

    def scatter_sum(partial_sum):
        return lax.psum_scatter(partial_sum, 'seq', scatter_dimension=0, tiled=True)

    def device_step(hidden, positions, g_attn, g_mlp, w_query, w_key, w_value, w_out, w_gate, w_up, w_down, d_out):
        batch_rows, tok_local, d_model = hidden.shape
        n_layers, unused_d, q_heads, head_dim = w_query.shape
        kv_heads = w_key.shape[2]
        q_group = q_heads // kv_heads
        halo_len = WINDOW - 1
        tail_start = tok_local - halo_len
        shard_idx = lax.axis_index('seq')
        key_start = jnp.where(shard_idx == 0, halo_len, 0)
        cos_t, sin_t = rope_tables(positions, head_dim)
        attend = functools.partial(window_attention, key_start=key_start)

        saved = []
        hidden_cur = hidden
        for layer_idx in range(n_layers):
            normed_a, unit_a, inv_a = rms_norm(hidden_cur, g_attn[layer_idx])
            q_proj = jnp.einsum('btd,dhe->bthe', normed_a, w_query[layer_idx], preferred_element_type=jnp.float32)
            k_proj = jnp.einsum('btd,dhe->bthe', normed_a, w_key[layer_idx], preferred_element_type=jnp.float32)
            v_proj = jnp.einsum('btd,dhe->bthe', normed_a, w_value[layer_idx], preferred_element_type=jnp.float32)
            q_rot = rotate(q_proj, cos_t, sin_t).astype(jnp.bfloat16).reshape(batch_rows, tok_local, kv_heads, q_group, head_dim)
            k_rot = rotate(k_proj, cos_t, sin_t).astype(jnp.bfloat16)
            v_val = v_proj.astype(jnp.bfloat16)
            k_recv = lax.ppermute(k_rot[:, tail_start:], 'seq', to_right)
            v_recv = lax.ppermute(v_val[:, tail_start:], 'seq', to_right)
            k_ext = jnp.concatenate([k_recv, k_rot], axis=1)
            v_ext = jnp.concatenate([v_recv, v_val], axis=1)
            attn_out, attn_pull = jax.vjp(attend, q_rot, k_ext, v_ext)
            attn_proj = jnp.einsum('btf,fd->btd', attn_out, w_out[layer_idx], preferred_element_type=jnp.float32)
            hidden_mid = (hidden_cur.astype(jnp.float32) + attn_proj).astype(jnp.bfloat16)
            normed_m, unit_m, inv_m = rms_norm(hidden_mid, g_mlp[layer_idx])
            gate_pre = jnp.einsum('btd,df->btf', normed_m, w_gate[layer_idx], preferred_element_type=jnp.float32)
            up_proj = jnp.einsum('btd,df->btf', normed_m, w_up[layer_idx], preferred_element_type=jnp.float32)
            act_prod = (jax.nn.silu(gate_pre) * up_proj).astype(jnp.bfloat16)
            down_proj = jnp.einsum('btf,fd->btd', act_prod, w_down[layer_idx], preferred_element_type=jnp.float32)
            saved.append(dict(normed_a=normed_a, unit_a=unit_a, inv_a=inv_a, attn_pull=attn_pull, attn_out=attn_out, normed_m=normed_m, unit_m=unit_m, inv_m=inv_m, gate_pre=gate_pre, up_proj=up_proj, act_prod=act_prod))
            hidden_cur = (hidden_mid.astype(jnp.float32) + down_proj).astype(jnp.bfloat16)

        grad_hidden = d_out
        per_layer = []
        for layer_idx in reversed(range(n_layers)):
            record = saved[layer_idx]
            grad_res = grad_hidden.astype(jnp.float32)
            dw_down_part = jnp.einsum('btf,btd->fd', record['act_prod'], grad_hidden, preferred_element_type=jnp.float32)
            grad_act = jnp.einsum('btd,fd->btf', grad_hidden, w_down[layer_idx], preferred_element_type=jnp.float32).astype(jnp.bfloat16).astype(jnp.float32)
            sig_gate = jax.nn.sigmoid(record['gate_pre'])
            grad_gate = (grad_act * record['up_proj'] * sig_gate * (1.0 + record['gate_pre'] * (1.0 - sig_gate))).astype(jnp.bfloat16)
            grad_up = (grad_act * record['gate_pre'] * sig_gate).astype(jnp.bfloat16)
            dw_gate_part = jnp.einsum('btd,btf->df', record['normed_m'], grad_gate, preferred_element_type=jnp.float32)
            dw_up_part = jnp.einsum('btd,btf->df', record['normed_m'], grad_up, preferred_element_type=jnp.float32)
            grad_norm_m = (jnp.einsum('btf,df->btd', grad_gate, w_gate[layer_idx], preferred_element_type=jnp.float32)
                           + jnp.einsum('btf,df->btd', grad_up, w_up[layer_idx], preferred_element_type=jnp.float32))
            grad_mid_f, dg_mlp_part = rms_norm_bwd(grad_norm_m, record['unit_m'], record['inv_m'], g_mlp[layer_idx])
            grad_mid = (grad_mid_f + grad_res).astype(jnp.bfloat16)
            dw_out_part = jnp.einsum('btf,btd->fd', record['attn_out'], grad_mid, preferred_element_type=jnp.float32)
            grad_attn = jnp.einsum('btd,fd->btf', grad_mid, w_out[layer_idx], preferred_element_type=jnp.float32).astype(jnp.bfloat16)
            grad_q, grad_k_ext, grad_v_ext = record['attn_pull'](grad_attn)
            k_back = lax.ppermute(grad_k_ext[:, :halo_len], 'seq', to_left)
            v_back = lax.ppermute(grad_v_ext[:, :halo_len], 'seq', to_left)
            grad_k = add_tail(grad_k_ext[:, halo_len:], k_back)
            grad_v = add_tail(grad_v_ext[:, halo_len:], v_back)
            grad_qf = rotate_back(grad_q.reshape(batch_rows, tok_local, q_heads, head_dim).astype(jnp.float32), cos_t, sin_t).astype(jnp.bfloat16)
            grad_kf = rotate_back(grad_k, cos_t, sin_t).astype(jnp.bfloat16)
            grad_vf = grad_v.astype(jnp.bfloat16)
            dw_query_part = jnp.einsum('btd,bthe->dhe', record['normed_a'], grad_qf, preferred_element_type=jnp.float32)
            dw_key_part = jnp.einsum('btd,bthe->dhe', record['normed_a'], grad_kf, preferred_element_type=jnp.float32)
            dw_value_part = jnp.einsum('btd,bthe->dhe', record['normed_a'], grad_vf, preferred_element_type=jnp.float32)
            grad_norm_a = (jnp.einsum('bthe,dhe->btd', grad_qf, w_query[layer_idx], preferred_element_type=jnp.float32)
                           + jnp.einsum('bthe,dhe->btd', grad_kf, w_key[layer_idx], preferred_element_type=jnp.float32)
                           + jnp.einsum('bthe,dhe->btd', grad_vf, w_value[layer_idx], preferred_element_type=jnp.float32))
            grad_in_f, dg_attn_part = rms_norm_bwd(grad_norm_a, record['unit_a'], record['inv_a'], g_attn[layer_idx])
            grad_hidden = (grad_in_f + grad_mid.astype(jnp.float32)).astype(jnp.bfloat16)
            layer_parts = (dg_attn_part, dg_mlp_part, dw_query_part, dw_key_part, dw_value_part, dw_out_part, dw_gate_part, dw_up_part, dw_down_part)
            per_layer.append([scatter_sum(partial_sum) for partial_sum in layer_parts])

        in_order = per_layer[::-1]
        stacked = tuple(jnp.stack([layer_grads[slot] for layer_grads in in_order]) for slot in range(9))
        return (grad_hidden,) + stacked

    tok_spec = P('data', 'seq', None)
    vec_spec = P(None, ('data', 'seq'))
    mat_spec = P(None, ('data', 'seq'), None)
    head_spec = P(None, ('data', 'seq'), None, None)
    in_specs = (tok_spec, P('data', 'seq'), P(), P(), P(), P(), P(), P(), P(), P(), P(), tok_spec)
    out_specs = (tok_spec, vec_spec, vec_spec, head_spec, head_spec, head_spec, mat_spec, mat_spec, mat_spec, mat_spec)
    return jax.shard_map(device_step, mesh=mesh, in_specs=in_specs, out_specs=out_specs, check_vma=False)
```

profile of v0, /device:TPU:97, one launch (start us, length us, event | category | flops | bytes accessed | tf_op | source)
XLA Modules:
  0.0 927.1 jit_solution(15909045943398669193)
XLA Ops:
  19.1 4.6 collective-permute-start.1
  29.7 10.1 %convolution_convert_fusion.1 = bf16[3,384,3072]{2,1,0:T(8,128)(2,1)} fusion(bf16[3,384,768]{2,1,0:T(8,128)(2,1)} %param.27, bf16[1,3072,768]{2,1,0:T(8,128)(2,1)} %param.26), kind=kOutput, calls=%fused_computation.96 | convolution fusion | flops 5439356928 | bytes 13565952 | tf_op jit(solution)/shard_map/btd,fd->btf/dot_general | solution.py:129
  39.9 4.4 maximum_maximum_fusion
  44.2 5.2 collective-permute-done
  49.4 4.2 pad_maximum_fusion
  53.6 32.9 %while.31 = (s32[]{:T(128)}, bf16[3,3,128,12,1,64]{2,5,3,1,4,0:T(8,128)(2,1)}, s32[3]{0:T(128)S(1)}, bf16[3,639,12,64]{1,3,2,0:T(8,128)(2,1)}, s32[]{:T(128)}, /...) while((s32[]{:T(128)}, ...), condition=%wide.region_4.5_spmd.clone, body=%wide.region_1.4_spmd.clone.sunk | while | flops 473466112 | bytes 37996284 | solution.py:67
  55.0 4.4 fusion.210
  66.0 4.4 fusion.210
  77.0 4.2 fusion.210
  86.6 4.6 copy.58
  91.2 5.6 reshape.253
  96.8 4.2 fusion.134
  102.3 11.2 %fusion.120 = f32[3,384,3072]{2,1,0:T(8,128)} fusion(bf16[1,768,3072]{2,1,0:T(8,128)(2,1)} %param.25, bf16[3,384,768]{2,1,0:T(8,128)(2,1)S(1)} %get-tuple-element.482, f32[768]{0:T(1024)S(1)} %reduce.30, f32[3,384]{1,0:T(4,128)S(1)} %add_rsqrt_fusion), kind=kOutput, calls=%fused_computation.113 | convolution fusion | flops 5439356928 | bytes 20651520 | tf_op jit(solution)/shard_map/btd,df->btf/dot_general | solution.py:117
  113.5 21.9 %fusion.107 = (bf16[3,384,3072]{2,1,0:T(8,128)(2,1)}, bf16[3,384,3072]{2,1,0:T(8,128)(2,1)}, f32[3,384,3072]{2,1,0:T(8,128)}) fusion(bf16[3,384,3072]{2,1,0:T(8,128)(2,1)} %convolution_convert_fusion.1, f32[3,384,3072]{2,1,0:T(8,128)} %fusion.120, bf16[1,768,3072]{2,1,0:T(8,128)(2,1)} %param.24, bf16[3,384,768]{2,1,0:T(8,128)(2,1)} %copy-done.22, ...), kind=kOutput, calls=%fused_computation.92 | convolution fusion | flops 5488902144 | bytes 56040960 | tf_op jit(solution)/shard_map/btd,df->btf/dot_general | solution.py:116
  135.4 9.9 %fusion.114 = f32[3,384,768]{2,1,0:T(8,128)S(1)} fusion(bf16[3,384,3072]{2,1,0:T(8,128)(2,1)} %get-tuple-element.466, bf16[1,768,3072]{2,1,0:T(8,128)(2,1)} %param.24), kind=kOutput, calls=%fused_computation.107 | convolution fusion | flops 5435817984 | bytes 15335424 | tf_op jit(solution)/shard_map/btf,df->btd/dot_general | solution.py:135
  145.4 9.7 %fusion.133 = (f32[768]{0:T(1024)}, f32[3,384]{1,0:T(4,128)S(1)}, f32[3,384,768]{2,1,0:T(8,128)S(1)}) fusion(bf16[3,384,768]{2,1,0:T(8,128)(2,1)S(1)} %copy-done.23, f32[3,384]{1,0:T(4,128)S(1)} %add_rsqrt_fusion, f32[768]{0:T(1024)S(1)} %reduce.30, f32[3,384,768]{2,1,0:T(8,128)S(1)} %fusion.114, bf16[3,384,3072]{2,1,0:T(8,128)(2,1)S(1)} %copy-done.50, ...), kind=kOutput, calls=%fused_computation.128 | convolution fusion | flops 5442893824 | bytes 20659200 | tf_op jit(solution)/shard_map/btf,df->btd/dot_general | solution.py:136
  166.2 5.6 reshape.254
  180.8 198.1 %while.32 = (s32[]{:T(128)}, bf16[3,384,12,1,64]{1,4,2,0,3:T(8,128)(2,1)}, bf16[3,639,12,64]{1,3,2,0:T(8,128)(2,1)}, bf16[3,639,12,64]{1,3,2,0:T(8,128)(2,1)}, s...) while((s32[]{:T(128)}, ...), condition=%wide.region_11.12_spmd.clone, body=%wide.region_7.11_spmd.clone.sunk | while | flops 1207073536 | bytes 188581648 | solution.py:67
  196.3 14.0 %add_any.59 = bf16[3,639,12,64]{1,3,2,0:T(8,128)(2,1)} dynamic-update-slice(bf16[3,639,12,64]{1,3,2,0:T(8,128)(2,1)} %get-tuple-element.691, bf16[3,383,12,64]{1,3,2,0:T(8,128)(2,1)S(1)} %bitcast_add_fusion.7, s32[]{:T(128)} %constant.171.clone.1..sunk.1, s32[]{:T(128)S(6)} %select_n.148, s32[]{:T(128)} %constant.171.clone.1..sunk.1, s32[]{:T(128)} %constant.171.clone.1..sunk.1) | dynamic-update-slice | bytes 3529732 | tf_op jit(solution)/shard_map/transpose(jvp())/while/body/eval_jaxpr/add_any | solution.py:67
  210.4 6.4 fusion.222
  218.5 5.4 bitcast_add_fusion.6
  223.9 14.0 %add_any.58 = bf16[3,639,12,64]{1,3,2,0:T(8,128)(2,1)} dynamic-update-slice(bf16[3,639,12,64]{1,3,2,0:T(8,128)(2,1)} %get-tuple-element.690, bf16[3,383,12,64]{1,3,2,0:T(8,128)(2,1)S(1)} %bitcast_add_fusion.6, s32[]{:T(128)} %constant.171.clone.1..sunk.1, s32[]{:T(128)S(6)} %select_n.148, s32[]{:T(128)} %constant.171.clone.1..sunk.1, s32[]{:T(128)} %constant.171.clone.1..sunk.1) | dynamic-update-slice | bytes 3529732 | tf_op jit(solution)/shard_map/transpose(jvp())/while/body/eval_jaxpr/add_any | solution.py:67
  237.9 7.9 fusion.223
  261.4 14.5 %add_any.59 = bf16[3,639,12,64]{1,3,2,0:T(8,128)(2,1)} dynamic-update-slice(bf16[3,639,12,64]{1,3,2,0:T(8,128)(2,1)} %get-tuple-element.691, bf16[3,383,12,64]{1,3,2,0:T(8,128)(2,1)S(1)} %bitcast_add_fusion.7, s32[]{:T(128)} %constant.171.clone.1..sunk.1, s32[]{:T(128)S(6)} %select_n.148, s32[]{:T(128)} %constant.171.clone.1..sunk.1, s32[]{:T(128)} %constant.171.clone.1..sunk.1) | dynamic-update-slice | bytes 3529732 | tf_op jit(solution)/shard_map/transpose(jvp())/while/body/eval_jaxpr/add_any | solution.py:67
  275.9 6.5 fusion.222
  284.1 5.4 bitcast_add_fusion.6
  289.5 14.5 %add_any.58 = bf16[3,639,12,64]{1,3,2,0:T(8,128)(2,1)} dynamic-update-slice(bf16[3,639,12,64]{1,3,2,0:T(8,128)(2,1)} %get-tuple-element.690, bf16[3,383,12,64]{1,3,2,0:T(8,128)(2,1)S(1)} %bitcast_add_fusion.6, s32[]{:T(128)} %constant.171.clone.1..sunk.1, s32[]{:T(128)S(6)} %select_n.148, s32[]{:T(128)} %constant.171.clone.1..sunk.1, s32[]{:T(128)} %constant.171.clone.1..sunk.1) | dynamic-update-slice | bytes 3529732 | tf_op jit(solution)/shard_map/transpose(jvp())/while/body/eval_jaxpr/add_any | solution.py:67
  304.0 8.0 fusion.223
  327.6 14.8 %add_any.59 = bf16[3,639,12,64]{1,3,2,0:T(8,128)(2,1)} dynamic-update-slice(bf16[3,639,12,64]{1,3,2,0:T(8,128)(2,1)} %get-tuple-element.691, bf16[3,383,12,64]{1,3,2,0:T(8,128)(2,1)S(1)} %bitcast_add_fusion.7, s32[]{:T(128)} %constant.171.clone.1..sunk.1, s32[]{:T(128)S(6)} %select_n.148, s32[]{:T(128)} %constant.171.clone.1..sunk.1, s32[]{:T(128)} %constant.171.clone.1..sunk.1) | dynamic-update-slice | bytes 3529732 | tf_op jit(solution)/shard_map/transpose(jvp())/while/body/eval_jaxpr/add_any | solution.py:67
  342.4 6.5 fusion.222
  350.6 5.4 bitcast_add_fusion.6
  356.1 14.8 %add_any.58 = bf16[3,639,12,64]{1,3,2,0:T(8,128)(2,1)} dynamic-update-slice(bf16[3,639,12,64]{1,3,2,0:T(8,128)(2,1)} %get-tuple-element.690, bf16[3,383,12,64]{1,3,2,0:T(8,128)(2,1)S(1)} %bitcast_add_fusion.6, s32[]{:T(128)} %constant.171.clone.1..sunk.1, s32[]{:T(128)S(6)} %select_n.148, s32[]{:T(128)} %constant.171.clone.1..sunk.1, s32[]{:T(128)} %constant.171.clone.1..sunk.1) | dynamic-update-slice | bytes 3529732 | tf_op jit(solution)/shard_map/transpose(jvp())/while/body/eval_jaxpr/add_any | solution.py:67
  370.9 8.0 fusion.223
  384.4 14.3 %collective-permute-done.3 = bf16[3,255,12,64]{1,3,2,0:T(8,128)(2,1)S(1)} collective-permute-done((bf16[3,255,12,64]{1,3,2,0:T(8,128)(2,1)S(1)}, bf16[3,255,12,64]{1,3,2,0:T(8,128)(2,1)S(1)}, u32[]{:S(2)}, u32[]{:S(2)}) %collective-permute-start.3) | collective-permute-done | bytes 1175072 | tf_op jit(solution)/shard_map/ppermute | solution.py:143
  401.5 6.4 convolution_bitcast_fusion.2
  413.9 13.2 %collective-permute-done.2 = bf16[3,255,12,64]{1,3,2,0:T(8,128)(2,1)S(1)} collective-permute-done((bf16[3,255,12,64]{1,3,2,0:T(8,128)(2,1)S(1)}, bf16[3,255,12,64]{1,3,2,0:T(8,128)(2,1)S(1)}, u32[]{:S(2)}, u32[]{:S(2)}) %collective-permute-start.2) | collective-permute-done | bytes 1175072 | tf_op jit(solution)/shard_map/ppermute | solution.py:142
  432.7 5.4 convolution_bitcast_fusion.3
  438.3 6.5 convolution_bitcast_fusion.4
  445.5 11.5 %convolution_bitcast_fusion.1 = f32[768,3072]{1,0:T(8,128)} fusion(bf16[3,384,3072]{2,1,0:T(8,128)(2,1)} %get-tuple-element.466, bf16[3,384,768]{2,1,0:T(8,128)(2,1)} %copy-done.22, f32[768]{0:T(1024)S(1)} %copy-done.43, f32[3,384]{1,0:T(4,128)S(1)} %copy-done.39), kind=kOutput, calls=%fused_computation.98 | convolution fusion | flops 5439356928 | bytes 18292224 | tf_op jit(solution)/shard_map/btd,btf->df/dot_general | solution.py:133
  457.1 11.5 %convolution_bitcast_fusion = f32[768,3072]{1,0:T(8,128)} fusion(bf16[3,384,3072]{2,1,0:T(8,128)(2,1)} %get-tuple-element.465, bf16[3,384,768]{2,1,0:T(8,128)(2,1)} %copy-done.22, f32[768]{0:T(1024)S(1)} %copy-done.43, f32[3,384]{1,0:T(4,128)S(1)} %copy-done.39), kind=kOutput, calls=%fused_computation.97 | convolution fusion | flops 5439356928 | bytes 18292224 | tf_op jit(solution)/shard_map/btd,btf->df/dot_general | solution.py:134
  468.7 15.7 %fusion.109 = f32[3072,768]{1,0:T(8,128)} fusion(bf16[3,384,768]{2,1,0:T(8,128)(2,1)} %param.27, f32[3,384,3072]{2,1,0:T(8,128)} %fusion.120, f32[3,384,3072]{2,1,0:T(8,128)} %get-tuple-element.483), kind=kOutput, calls=%fused_computation.99 | convolution fusion | flops 5457051648 | bytes 39518208 | tf_op jit(solution)/shard_map/btf,btd->fd/dot_general | solution.py:128
  489.8 4.7 fusion.141
  494.5 51.3 %all-reduce.2 = (f32[768]{0:T(1024)S(1)}, f32[768]{0:T(1024)S(1)}) all-reduce(f32[768]{0:T(1024)S(1)} %get-tuple-element.417, f32[768]{0:T(1024)S(1)} %copy-done.45), channel_id=2, replica_groups=mesh['data'=1,'seq'=32] {'seq'}, use_global_device_ids=true, to_apply=%region_14.15.clone | all-reduce | flops 1536 | bytes 12288
  550.4 16.3 %reduce-scatter.10.cloned.1.call-done = f32[24,12,64]{2,0,1:T(8,128)} async-done(((f32[768,12,64]{2,0,1:T(8,128)}), f32[24,12,64]{2,0,1:T(8,128)}) %reduce-scatter.10.cloned.1.call-update) | async-done | bytes 73744 | tf_op jit(solution)/shard_map/reduce_scatter | solution.py:84
  566.7 79.6 %reduce-scatter.8.cloned.1.call-done = f32[24,12,64]{2,0,1:T(8,128)} async-done(((f32[768,12,64]{2,0,1:T(8,128)}), f32[24,12,64]{2,0,1:T(8,128)}) %reduce-scatter.8.cloned.1.call-update) | async-done | bytes 73744 | tf_op jit(solution)/shard_map/reduce_scatter | solution.py:84
  646.3 91.1 %reduce-scatter.16.cloned.1.call-done = f32[24,3072]{1,0:T(8,128)} async-done(((f32[768,3072]{1,0:T(8,128)}), f32[24,3072]{1,0:T(8,128)}) %reduce-scatter.16.cloned.1.call-update) | async-done | bytes 294928 | tf_op jit(solution)/shard_map/reduce_scatter | solution.py:84
  737.5 91.2 %reduce-scatter.18.cloned.1.call-done = f32[24,3072]{1,0:T(8,128)} async-done(((f32[768,3072]{1,0:T(8,128)}), f32[24,3072]{1,0:T(8,128)}) %reduce-scatter.18.cloned.1.call-update) | async-done | bytes 294928 | tf_op jit(solution)/shard_map/reduce_scatter | solution.py:84
  828.7 91.3 %reduce-scatter.20.cloned.1.call-done = f32[96,768]{1,0:T(8,128)} async-done(((f32[3072,768]{1,0:T(8,128)}), f32[96,768]{1,0:T(8,128)}) %reduce-scatter.20.cloned.1.call-update) | async-done | bytes 294928 | tf_op jit(solution)/shard_map/reduce_scatter | solution.py:84
  (249 shorter events, 136.9 us)
Async XLA Ops:
  7.2 16.5 %copy-start = (bf16[1,768,12,64]{1,3,2,0:T(8,128)(2,1)S(1)}, bf16[1,768,12,64]{1,3,2,0:T(8,128)(2,1)}, u32[]{:S(2)}) copy-start(bf16[1,768,12,64]{1,3,2,0:T(8,128)(2,1)} %param.22) | copy-start | bytes 3538948
  7.2 543.2 %reduce-scatter.14.cloned.1.call-start = ((), (), s32[]{:S(2)}) async-start(), calls=%async_computation.10 | async-start | bytes 2433024 | tf_op jit(solution)/shard_map/reduce_scatter | solution.py:84
  9.3 14.4 %copy-start.36 = (f32[3,384]{1,0:T(4,128)}, f32[3,384]{1,0:T(4,128)S(1)}, u32[]{:S(2)}) copy-start(f32[3,384]{1,0:T(4,128)S(1)} %add_rsqrt_fusion.1) | copy-start | bytes 13828
  10.0 13.7 %copy-start.40 = (f32[768]{0:T(1024)}, f32[768]{0:T(1024)S(1)}, u32[]{:S(2)}) copy-start(f32[768]{0:T(1024)S(1)} %reduce.29) | copy-start | bytes 9220
  17.5 8.1 copy-start.8
  17.5 8.1 copy-start.10
  19.1 20.8 %collective-permute-start.1 = (bf16[3,255,12,64]{1,3,2,0:T(8,128)(2,1)}, bf16[3,255,12,64]{1,3,2,0:T(8,128)(2,1)}, u32[]{:S(2)}, u32[]{:S(2)}) collective-permute-start(bf16[3,255,12,64]{1,3,2,0:T(8,128)(2,1)} %pad_maximum_fusion.6), channel_id=1, source_target_pairs={{0,1},{1,2},{2,3},{3,4},{4,5},{5,6},{6,7},{7,8},{8,9},{9,10},{10,1... | collective-permute-start | bytes 3525128 | tf_op jit(solution)/shard_map/ppermute | solution.py:108
  25.6 4.1 copy-start.46
  27.1 22.3 %collective-permute-start = (bf16[3,255,12,64]{1,3,2,0:T(8,128)(2,1)}, bf16[3,255,12,64]{1,3,2,0:T(8,128)(2,1)}, u32[]{:S(2)}, u32[]{:S(2)}) collective-permute-start(bf16[3,255,12,64]{1,3,2,0:T(8,128)(2,1)} %slice.70), channel_id=1, source_target_pairs={{0,1},{1,2},{2,3},{3,4},{4,5},{5,6},{6,7},{7,8},{8,9},{9,10},{10,1... | collective-permute-start | bytes 3525128 | tf_op jit(solution)/shard_map/ppermute | solution.py:109
  29.7 125.4 %copy-start.42 = (f32[768]{0:T(1024)}, f32[768]{0:T(1024)S(1)}, u32[]{:S(2)}) copy-start(f32[768]{0:T(1024)S(1)} %reduce.30) | copy-start | bytes 9220
  29.7 10.2 %copy-start.9 = (bf16[3,384,12,32]{1,3,2,0:T(8,128)(2,1)S(1)}, bf16[3,384,12,32]{1,3,2,0:T(8,128)(2,1)}, u32[]{:S(2)}) copy-start(bf16[3,384,12,32]{1,3,2,0:T(8,128)(2,1)} %copy-done.8) | copy-start | bytes 2654212
  29.7 10.2 %copy-start.11 = (bf16[3,384,12,32]{1,3,2,0:T(8,128)(2,1)S(1)}, bf16[3,384,12,32]{1,3,2,0:T(8,128)(2,1)}, u32[]{:S(2)}) copy-start(bf16[3,384,12,32]{1,3,2,0:T(8,128)(2,1)} %copy-done.10) | copy-start | bytes 2654212
  39.8 9.6 %copy-start.18 = (bf16[3,384,12,64]{1,3,2,0:T(8,128)(2,1)S(1)}, bf16[3,384,12,64]{1,3,2,0:T(8,128)(2,1)}, u32[]{:S(2)}) copy-start(bf16[3,384,12,64]{1,3,2,0:T(8,128)(2,1)} %copy-done.17) | copy-start | bytes 5308420
  101.0 54.1 %copy-start.38 = (f32[3,384]{1,0:T(4,128)}, f32[3,384]{1,0:T(4,128)S(1)}, u32[]{:S(2)}) copy-start(f32[3,384]{1,0:T(4,128)S(1)} %add_rsqrt_fusion) | copy-start | bytes 13828
  135.4 10.0 %copy-start.23 = (bf16[3,384,768]{2,1,0:T(8,128)(2,1)S(1)}, bf16[3,384,768]{2,1,0:T(8,128)(2,1)}, u32[]{:S(2)}) copy-start(bf16[3,384,768]{2,1,0:T(8,128)(2,1)} %copy-done.22) | copy-start | bytes 5308420
  135.4 10.0 %copy-start.50 = (bf16[3,384,3072]{2,1,0:T(8,128)(2,1)S(1)}, bf16[3,384,3072]{2,1,0:T(8,128)(2,1)}, u32[]{:S(2)}) copy-start(bf16[3,384,3072]{2,1,0:T(8,128)(2,1)} %get-tuple-element.465) | copy-start | bytes 21233668
  145.4 9.7 %copy-start.21 = (bf16[3,384,768]{2,1,0:T(8,128)(2,1)S(1)}, bf16[3,384,768]{2,1,0:T(8,128)(2,1)}, u32[]{:S(2)}) copy-start(bf16[3,384,768]{2,1,0:T(8,128)(2,1)} %param.27) | copy-start | bytes 5308420
  175.2 375.3 %reduce-scatter.12.cloned.1.call-start = ((), (), s32[]{:S(2)}) async-start(), calls=%async_computation.9 | async-start | bytes 4866048 | tf_op jit(solution)/shard_map/reduce_scatter | solution.py:84
  180.9 7.6 copy-start.3
  188.5 4.6 copy-start.7
  210.3 8.1 copy-start.2
  210.4 8.1 copy-start.6
  237.9 7.9 copy-start.4
  245.8 7.7 copy-start.3
  253.6 4.6 copy-start.7
  275.9 8.2 copy-start.2
  275.9 8.2 copy-start.6
  304.0 8.0 copy-start.4
  312.0 7.7 copy-start.3
  319.8 4.6 copy-start.7
  342.4 8.2 copy-start.2
  342.4 8.2 copy-start.6
  370.9 8.0 copy-start.4
  380.2 21.3 %copy-start.14 = (bf16[3,384,768]{2,1,0:T(8,128)(2,1)S(1)}, bf16[3,384,768]{2,1,0:T(8,128)(2,1)}, u32[]{:S(2)}) copy-start(bf16[3,384,768]{2,1,0:T(8,128)(2,1)} %param.16) | copy-start | bytes 5308420
  380.3 21.3 %copy-start.37 = (f32[3,384]{1,0:T(4,128)S(1)}, f32[3,384]{1,0:T(4,128)}, u32[]{:S(2)}) copy-start(f32[3,384]{1,0:T(4,128)} %copy-done.36) | copy-start | bytes 13828
  380.3 21.2 %copy-start.41 = (f32[768]{0:T(1024)S(1)}, f32[768]{0:T(1024)}, u32[]{:S(2)}) copy-start(f32[768]{0:T(1024)} %copy-done.40) | copy-start | bytes 9220
  380.3 18.4 %collective-permute-start.3 = (bf16[3,255,12,64]{1,3,2,0:T(8,128)(2,1)S(1)}, bf16[3,255,12,64]{1,3,2,0:T(8,128)(2,1)S(1)}, u32[]{:S(2)}, u32[]{:S(2)}) collective-permute-start(bf16[3,255,12,64]{1,3,2,0:T(8,128)(2,1)S(1)} %slice.69), channel_id=1, source_target_pairs={{1,0},{2,1},{3,2},{4,3},{5,4},{6,5},{7,6},{8,7},{9,8},{10,9},{11,1... | collective-permute-start | bytes 3525128 | tf_op jit(solution)/shard_map/ppermute | solution.py:143
  384.4 16.1 %copy-start.30 = (bf16[3,129,12,64]{1,3,2,0:T(8,128)(2,1)}, bf16[3,129,12,64]{1,3,2,0:T(8,128)(2,1)S(1)}, u32[]{:S(2)}) copy-start(bf16[3,129,12,64]{1,3,2,0:T(8,128)(2,1)S(1)} %slice.67) | copy-start | bytes 1783300
  407.9 5.5 copy-start.12
  407.9 158.8 %reduce-scatter.10.cloned.1.call-start = ((), (), s32[]{:S(2)}) async-start(), calls=%async_computation.8 | async-start | bytes 4866048 | tf_op jit(solution)/shard_map/reduce_scatter | solution.py:84
  409.5 17.6 %collective-permute-start.2 = (bf16[3,255,12,64]{1,3,2,0:T(8,128)(2,1)S(1)}, bf16[3,255,12,64]{1,3,2,0:T(8,128)(2,1)S(1)}, u32[]{:S(2)}, u32[]{:S(2)}) collective-permute-start(bf16[3,255,12,64]{1,3,2,0:T(8,128)(2,1)S(1)} %slice.64), channel_id=1, source_target_pairs={{1,0},{2,1},{3,2},{4,3},{5,4},{6,5},{7,6},{8,7},{9,8},{10,9},{11,1... | collective-permute-start | bytes 3525128 | tf_op jit(solution)/shard_map/ppermute | solution.py:142
  413.9 14.9 %copy-start.25 = (f32[3,384,32]{1,2,0:T(8,128)S(1)}, f32[3,384,32]{1,2,0:T(8,128)}, u32[]{:S(2)}) copy-start(f32[3,384,32]{1,2,0:T(8,128)} %copy-done.24) | copy-start | bytes 442372
  413.9 14.9 %copy-start.27 = (f32[3,384,32]{1,2,0:T(8,128)S(1)}, f32[3,384,32]{1,2,0:T(8,128)}, u32[]{:S(2)}) copy-start(f32[3,384,32]{1,2,0:T(8,128)} %copy-done.26) | copy-start | bytes 442372
  438.2 208.2 %reduce-scatter.8.cloned.1.call-start = ((), (), s32[]{:S(2)}) async-start(), calls=%async_computation.7 | async-start | bytes 4866048 | tf_op jit(solution)/shard_map/reduce_scatter | solution.py:84
  444.9 292.6 %reduce-scatter.16.cloned.1.call-start = ((), (), s32[]{:S(2)}) async-start(), calls=%async_computation.11 | async-start | bytes 9732096 | tf_op jit(solution)/shard_map/reduce_scatter | solution.py:84
  457.1 371.6 %reduce-scatter.18.cloned.1.call-start = ((), (), s32[]{:S(2)}) async-start(), calls=%async_computation.12 | async-start | bytes 9732096 | tf_op jit(solution)/shard_map/reduce_scatter | solution.py:84
  468.7 451.3 %reduce-scatter.20.cloned.1.call-start = ((), (), s32[]{:S(2)}) async-start(), calls=%async_computation.13 | async-start | bytes 9732096 | tf_op jit(solution)/shard_map/reduce_scatter | solution.py:84
  489.7 4.8 copy-start.45
  (33 other events, 78.6 us)
Sparse Core Ops, SparseCore 0:
  175.3 73.7 reduce-scatter.13
  408.0 78.5 reduce-scatter.11
  490.8 75.8 reduce-scatter.9
  570.7 75.6 reduce-scatter.7
  650.4 87.0 reduce-scatter.15
  741.5 87.1 reduce-scatter.17
  832.8 87.1 reduce-scatter.19
where the time goes:
time: 937 us; the launch traced here: 927 us
  waiting for transfers between devices  403 us (43%)
  matrix products  251 us (27%)
  local copies, waits for them, and re-layouts  150 us (16%)
  blocking collectives  51.3 us (5%)
  other arithmetic  41.4 us (4%)
  between operations  15.1 us (2%)
  starting transfers between devices  11.2 us (1%)
    reduce_scatter x7, waiting for transfers between devices, scatter_sum(): return lax.psum_scatter(partial_sum, 'seq', scatter_dimension=0, tiled=True)  370 us
    add_any x6, local copies, waits for them, and re-layouts, window_attention(): blocks = lax.map(jax.checkpoint(one_block), jnp.arange(tok_local // qblock))  86.6 us
    dot_general x12, matrix products, one_block(): jnp.einsum('bqkgd,bckd->bkgqc', q_blk, k_blk, preferred_element_type=jnp....  64.8 us
    unnamed x1, blocking collectives  51.3 us
    dot_general x9, matrix products, one_block(): jnp.einsum('bkgqc,bckd->bqkgd', attn_probs, v_blk, preferred_element_type...  39.1 us
    dot_general x1, matrix products, device_step(): jnp.einsum('btd,df->btf', normed_m, w_gate[layer_idx], preferred_element_...  21.9 us
  transfers between devices with their start and end apart: 11, of which 8 were waited for; matrix products, arithmetic and copies ran while one was open for 32% of the time, Pallas kernels for 0%

commit v1 on v0

v1 whole, which is shorter than its diff:
```python
import functools, math
import numpy as np
import jax, jax.numpy as jnp
from jax import lax
from jax.experimental import pallas as pl
from jax.experimental.pallas import tpu as pltpu
from jax.sharding import PartitionSpec as P

WINDOW = 256
NORM_EPS = 1e-5
QB = 128
BF, F32 = jnp.bfloat16, jnp.float32
NN, NT, TN = ((1,), (0,)), ((1,), (1,)), ((0,), (0,))
MESH = pl.DeviceIdType.MESH
NEG = -1e30
VMEM_LIMIT = 67043328


def dot(a, b, dims=NN):
    return lax.dot_general(a, b, (dims, ((), ())), preferred_element_type=F32)


def cdiv_loop(n, body):
    lax.fori_loop(0, n, lambda i, c: (body(i), c)[1], 0)


def rope(blk, cos_b, sin_b, sign, head_dim):
    half = head_dim // 2
    parts = []
    for h in range(blk.shape[0] // head_dim):
        first = blk[h * head_dim:h * head_dim + half]
        second = blk[h * head_dim + half:(h + 1) * head_dim]
        if sign > 0:
            parts += [first * cos_b - second * sin_b, second * cos_b + first * sin_b]
        else:
            parts += [first * cos_b + second * sin_b, second * cos_b - first * sin_b]
    return jnp.concatenate(parts, axis=0)


def normed(x, gain):
    xf = x.astype(F32)
    inv = lax.rsqrt(jnp.mean(xf * xf, axis=-1, keepdims=True) + NORM_EPS)
    return (xf * inv * gain).astype(BF)


def stack_pair(pair_t):
    half = pair_t.shape[0] // 2
    zero = jnp.zeros((half, pair_t.shape[1]), pair_t.dtype)
    return jnp.concatenate(
        [jnp.concatenate([pair_t[:half], zero], axis=0), jnp.concatenate([zero, pair_t[half:]], axis=0)], axis=1)


def unstack_pair(both):
    half, cols = both.shape[0] // 2, both.shape[1] // 2
    return jnp.concatenate([both[:half, :cols], both[half:, cols:]], axis=0)


def probs(k_blk, q_stack, upper, bias0, bias1):
    scores = dot(k_blk, q_stack)
    s02 = jnp.where(upper, scores[:QB] + bias0, scores[2 * QB:])
    s1 = scores[QB:2 * QB] + bias1
    top = jnp.max(jnp.maximum(s02, s1), axis=0, keepdims=True)
    e02, e1 = jnp.exp(s02 - top), jnp.exp(s1 - top)
    inv = 1.0 / jnp.sum(e02 + e1, axis=0, keepdims=True)
    return e02 * inv, e1 * inv


def banded(p02, p1, upper):
    return jnp.concatenate(
        [jnp.where(upper, p02, 0.0).astype(BF), p1.astype(BF), jnp.where(upper, 0.0, p02).astype(BF)], axis=0)


def upper_mask():
    key_ids = lax.broadcasted_iota(jnp.int32, (QB, 2 * QB), 0)
    query_ids = lax.broadcasted_iota(jnp.int32, (QB, 2 * QB), 1) % QB
    return key_ids > query_ids


def start_bias(first, blk):
    bias = jnp.where(first, NEG, 0.0).astype(F32)
    return (bias if blk < 2 else 0.0), (bias if blk < 1 else 0.0)


def fwd_kernel(n, head_dim, x_h, pos, invf, ga, gm, wq_h, wk_h, wv_h, wo_h,
               q_h, kt_h, k_h, v_h, hat_h, ot_h, xm_h, hm_h, hmt_h, cos_t, sin_t,
               xv, halo, pos_halo, wq, wk, wv, wo, q, kt, k, v, vt, hat, ot, xm, hm, hmt, hb, acc, cos_h, sin_h,
               ld, st, snd, rcv):
    rows, toks, width = xv.shape
    ext = toks + WINDOW
    total, n_halo = rows * toks, rows * WINDOW
    n_pairs = wq.shape[0] // (2 * head_dim)
    pw = 2 * head_dim
    me = lax.axis_index("seq")
    right, left = lax.rem(me + 1, n), lax.rem(me + n - 1, n)
    loads = [pltpu.make_async_copy(s, d, ld.at[i]) for i, (s, d) in enumerate(((x_h, xv), (wq_h, wq), (wk_h, wk), (wv_h, wv), (wo_h, wo)))]
    for c in loads:
        c.start()
    barrier = pltpu.get_barrier_semaphore()
    for other in (left, right):
        pl.semaphore_signal(barrier, inc=1, device_id={"seq": other}, device_id_type=MESH)
    pl.semaphore_wait(barrier, 2)
    sends = [pltpu.make_async_remote_copy(src_ref=s, dst_ref=d, send_sem=snd.at[i], recv_sem=rcv.at[i], device_id={"seq": right}, device_id_type=MESH)
             for i, (s, d) in enumerate(((x_h.at[:, toks - WINDOW:, :], halo), (pos, pos_halo)))]
    for c in sends:
        c.start()

    def store(i, s, d):
        c = pltpu.make_async_copy(s, d, st.at[i])
        c.start()
        stores.append(c)

    stores = []
    for b in range(rows):
        ang = invf[...] * pos[b:b + 1, :].astype(F32)
        cos_t[:, b * toks:(b + 1) * toks] = jnp.cos(ang)
        sin_t[:, b * toks:(b + 1) * toks] = jnp.sin(ang)
    loads[0].wait()
    tb = toks // QB

    def norm_blk(i):
        r = pl.multiple_of(i * QB, QB)
        h = normed(xv[i // tb, pl.ds(pl.multiple_of((i % tb) * QB, QB), QB), :], ga[...])
        hb[pl.ds(r, QB), :] = h
        hat[:, pl.ds(r, QB)] = h.T

    cdiv_loop(total // QB, norm_blk)
    store(0, hat, hat_h)

    def rope_q(p):
        r = pl.multiple_of(p * pw, pw)
        q[pl.ds(r, pw), :] = (rope(acc[pl.ds(r, pw), :], cos_t[...], sin_t[...], 1, head_dim) * (head_dim ** -0.5)).astype(BF)

    def put_k(p):
        r = pl.multiple_of(p * pw, pw)
        for b in range(rows):
            blk = rope(acc[pl.ds(r, pw), b * toks:(b + 1) * toks], cos_t[:, b * toks:(b + 1) * toks], sin_t[:, b * toks:(b + 1) * toks], 1, head_dim).astype(BF)
            kt[pl.ds(r, pw), b * ext + WINDOW:(b + 1) * ext] = blk
            k[b * ext + WINDOW:(b + 1) * ext, pl.ds(r, pw)] = blk.T

    def put_v(p):
        r = pl.multiple_of(p * pw, pw)
        for b in range(rows):
            blk = acc[pl.ds(r, pw), b * toks:(b + 1) * toks].astype(BF)
            vt[pl.ds(r, pw), b * ext + WINDOW:(b + 1) * ext] = blk
            v[b * ext + WINDOW:(b + 1) * ext, pl.ds(r, pw)] = blk.T

    for i, (w, put) in enumerate(((wq, rope_q), (wk, put_k), (wv, put_v))):
        loads[i + 1].wait()
        acc[...] = dot(w[...], hb[...], NT)
        cdiv_loop(n_pairs, put)
    store(1, q, q_h)

    for c in sends:
        c.wait()
    for b in range(rows):
        ang = invf[...] * pos_halo[b:b + 1, toks - WINDOW:].astype(F32)
        cos_h[:, b * WINDOW:(b + 1) * WINDOW] = jnp.cos(ang)
        sin_h[:, b * WINDOW:(b + 1) * WINDOW] = jnp.sin(ang)
    wb = WINDOW // QB

    def norm_halo(i):
        h = normed(halo[i // wb, pl.ds(pl.multiple_of((i % wb) * QB, QB), QB), :], ga[...])
        hb[pl.ds(pl.multiple_of(i * QB, QB), QB), :] = h

    cdiv_loop(n_halo // QB, norm_halo)

    def halo_put(is_k, p):
        r = pl.multiple_of(p * pw, pw)
        for b in range(rows):
            blk = acc[pl.ds(r, pw), b * WINDOW:(b + 1) * WINDOW]
            if is_k:
                blk = rope(blk, cos_h[:, b * WINDOW:(b + 1) * WINDOW], sin_h[:, b * WINDOW:(b + 1) * WINDOW], 1, head_dim)
            blk = blk.astype(BF)
            dst_t, dst = (kt, k) if is_k else (vt, v)
            dst_t[pl.ds(r, pw), b * ext:b * ext + WINDOW] = blk
            dst[b * ext:b * ext + WINDOW, pl.ds(r, pw)] = blk.T

    for w, is_k in ((wk, True), (wv, False)):
        acc[:, :n_halo] = dot(w[...], hb[:n_halo, :], NT)
        cdiv_loop(n_pairs, functools.partial(halo_put, is_k))
    store(2, kt, kt_h)
    store(3, k, k_h)
    store(4, v, v_h)

    upper = upper_mask()
    first = me == 0

    def attend(it):
        p, b = it // rows, it % rows
        r = pl.multiple_of(p * pw, pw)
        for blk in range(tb):
            cols = pl.ds(pl.multiple_of(b * toks + blk * QB, QB), QB)
            keys = pl.ds(pl.multiple_of(b * ext + blk * QB, QB), 3 * QB)
            bias0, bias1 = start_bias(first, blk)
            p02, p1 = probs(k[keys, pl.ds(r, pw)], stack_pair(q[pl.ds(r, pw), cols]), upper, bias0, bias1)
            out = dot(vt[pl.ds(r, pw), keys], banded(p02, p1, upper))
            ot[pl.ds(r, pw), cols] = unstack_pair(out).astype(BF)

    cdiv_loop(n_pairs * rows, attend)
    store(5, ot, ot_h)
    loads[4].wait()

    def project(b):
        cols = pl.ds(pl.multiple_of(b * toks, QB), toks)
        mid = (xv[b].astype(F32) + dot(ot[:, cols], wo[...], TN)).astype(BF)
        xm[cols, :] = mid
        h = normed(mid, gm[...])
        hm[cols, :] = h
        hmt[:, cols] = h.T

    cdiv_loop(rows, project)
    store(6, xm, xm_h)
    store(7, hm, hm_h)
    store(8, hmt, hmt_h)
    for c in stores:
        c.wait()


def any_spec(k):
    return [pl.BlockSpec(memory_space=pl.ANY)] * k


def vmem_spec(k):
    return [pl.BlockSpec(memory_space=pltpu.VMEM)] * k


def run_fwd(n, x, pos, invf, ga, gm, wq, wk, wv, wo, head_dim):
    rows, toks, width = x.shape
    hd = wq.shape[0]
    ext, total, n_halo = toks + WINDOW, rows * toks, rows * WINDOW
    half = head_dim // 2
    sds = lambda *s: jax.ShapeDtypeStruct(s, BF)
    outs = [sds(hd, total), sds(hd, rows * ext), sds(rows * ext, hd), sds(rows * ext, hd), sds(width, total), sds(hd, total), sds(total, width), sds(total, width), sds(width, total)]
    outs += [jax.ShapeDtypeStruct((half, total), F32)] * 2
    vm = lambda *s: pltpu.VMEM(s, BF)
    vf = lambda *s: pltpu.VMEM(s, F32)
    scratch = [vm(rows, toks, width), vm(rows, WINDOW, width), pltpu.VMEM((rows, toks), jnp.int32), vm(hd, width), vm(hd, width), vm(hd, width), vm(hd, width),
               vm(hd, total), vm(hd, rows * ext), vm(rows * ext, hd), vm(rows * ext, hd), vm(hd, rows * ext), vm(width, total), vm(hd, total), vm(total, width), vm(total, width), vm(width, total), vm(total, width),
               vf(hd, total), vf(half, n_halo), vf(half, n_halo),
               pltpu.SemaphoreType.DMA((5,)), pltpu.SemaphoreType.DMA((9,)), pltpu.SemaphoreType.DMA((2,)), pltpu.SemaphoreType.DMA((2,))]
    return pl.pallas_call(
        functools.partial(fwd_kernel, n, head_dim), out_shape=outs,
        in_specs=any_spec(1) + vmem_spec(4) + any_spec(4), out_specs=any_spec(9) + vmem_spec(2), scratch_shapes=scratch,
        compiler_params=pltpu.CompilerParams(collective_id=0, has_side_effects=True, vmem_limit_bytes=VMEM_LIMIT),
        name="forward")(x, pos, invf, ga, gm, wq, wk, wv, wo)


LAG = 2
SLOTS = 2 * LAG
RING = 5
CB = 256


def at(ref, *idx):
    return ref.at[idx]


class Torus:
    def __init__(self, n, pairs, odd_pair, parts, recv0, recv1, recv2, recv3, recv4, acc, acc2, fin, snd, rcv):
        self.side = math.isqrt(n // 2)
        assert self.side == 4
        me = lax.axis_index("seq")
        self.core = me % 2
        chip = me // 2
        self.x, self.y = chip % 4, chip // 4
        self.pairs, self.odd_pair = pairs, odd_pair
        self.parts, self.recv0, self.recv1, self.recv2, self.recv3, self.recv4 = parts, recv0, recv1, recv2, recv3, recv4
        self.acc, self.acc2, self.fin, self.snd, self.rcv = acc, acc2, fin, snd, rcv

    def device(self, dy, dx, flip=False):
        core = 1 - self.core if flip else self.core
        return (((self.y + dy) % 4) * 4 + (self.x + dx) % 4) * 2 + core

    def peers(self):
        return [self.device(0, 0, True), self.device(0, 1), self.device(0, 3), self.device(1, 0), self.device(3, 0)]

    def hop(self, kind, axis, step):
        return self.device(0, step) if (axis == kind) else self.device(step, 0)

    def copy(self, lane, kind, slot, src, dst, target):
        return pltpu.make_async_remote_copy(
            src_ref=src, dst_ref=dst, send_sem=self.snd.at[lane, kind, slot], recv_sem=self.rcv.at[lane, kind, slot],
            device_id={"seq": target}, device_id_type=MESH)

    def copies(self, stage, kind, pair, slot):
        held = pair % SLOTS
        if stage == 0:
            src = self.parts.at[pair % RING, kind, :, 1 - self.core]
            return [self.copy(0, kind, slot, src, self.recv0.at[kind, slot], self.device(0, 0, True))]
        axis = 0 if stage < 3 else 1
        plus, minus = self.hop(kind, axis, 1), self.hop(kind, axis, 3)
        if stage == 1:
            ends = [(self.acc.at[kind, held, 2, pl.ds(0, 2)], self.recv1), (self.acc.at[kind, held, 2, pl.ds(2, 2)], self.recv1)]
        elif stage == 2:
            ends = [(self.acc.at[kind, held, 1], self.recv2), (self.acc.at[kind, held, 3], self.recv2)]
        elif stage == 3:
            half = CB // 2
            ends = [(self.acc2.at[kind, held, 2, :, pl.ds(0, half)], self.recv3), (self.acc2.at[kind, held, 2, :, pl.ds(half, half)], self.recv3)]
        else:
            ends = [(self.acc2.at[kind, held, 1], self.recv4), (self.acc2.at[kind, held, 3], self.recv4)]
        lane = 2 * stage - 1
        return [self.copy(lane + i, kind, slot, src, buf.at[kind, slot, i], (plus, minus)[i]) for i, (src, buf) in enumerate(ends)]

    def add(self, stage, kind, pair, slot):
        held = pair % SLOTS
        acc, acc2 = self.acc, self.acc2
        if stage == 1:
            def row(r1):
                for r2 in range(4):
                    ry, rx = (r2, r1) if kind == 0 else (r1, r2)
                    chip = ((self.y + ry) % 4) * 4 + (self.x + rx) % 4
                    acc[kind, held, r1, r2] = self.parts[pair % RING, kind, chip, self.core] + self.recv0[kind, slot, chip]
            cdiv_loop(4, row)
        elif stage == 2:
            acc[kind, held, 1, 0:2] += self.recv1[kind, slot, 0]
            acc[kind, held, 3, 2:4] += self.recv1[kind, slot, 1]
        elif stage == 3:
            acc2[kind, held] = acc[kind, held, 0] + (self.recv2[kind, slot, 0] + self.recv2[kind, slot, 1])
        elif stage == 4:
            half = CB // 2
            acc2[kind, held, 1, :, 0:half] += self.recv3[kind, slot, 0]
            acc2[kind, held, 3, :, half:] += self.recv3[kind, slot, 1]
        else:
            self.fin[2 * pair + kind] = acc2[kind, held, 0] + (self.recv4[kind, slot, 0] + self.recv4[kind, slot, 1])

    def count(self, kind):
        return self.pairs - (1 if kind == 1 and self.odd_pair else 0)

    def when(self, pair, kind, fn):
        if isinstance(pair, int):
            if 0 <= pair < self.count(kind):
                fn()
        else:
            pl.when((pair >= 0) & (pair < self.count(kind)))(fn)

    def tick(self, t):
        for stage in range(5, 0, -1):
            pair = t - LAG * stage
            for kind in (0, 1):
                def take(stage=stage, pair=pair, kind=kind):
                    slot = (t - LAG) % SLOTS
                    for c in self.copies(stage - 1, kind, pair, slot):
                        c.wait()
                    self.add(stage, kind, pair, slot)
                self.when(pair, kind, take)
        for stage in range(4, -1, -1):
            pair = t - LAG * stage
            for kind in (0, 1):
                def give(stage=stage, pair=pair, kind=kind):
                    for c in self.copies(stage, kind, pair, t % SLOTS):
                        c.start()
                self.when(pair, kind, give)


def norm_back(x, gain, grad, res):
    xf = x.astype(F32)
    inv = lax.rsqrt(jnp.mean(xf * xf, axis=-1, keepdims=True) + NORM_EPS)
    unit = xf * inv
    gu = grad * gain
    out = inv * (gu - unit * jnp.mean(gu * unit, axis=-1, keepdims=True)) + res.astype(F32)
    gu = grad * unit
    return out.astype(BF), jnp.sum(gu.reshape(gu.shape[0] // 8, 8, gu.shape[1]), axis=0)


def bwd_kernel(n, head_dim, dims, ga, gm, x_h, dout_h, q_h, kt_h, k_h, v_h, hat_h, ot_h, xm_h, hm_h, hmt_h, cos_i, sin_i,
               wq_h, wk_h, wv_h, wo_h, wg_h, wu_h, wd_h,
               dx_h, dga_o, dgm_o, dq_o, dk_o, dv_o, do_o, dg_o, du_o, dd_o,
               parts, recv0, recv1, recv2, recv3, recv4, acc, acc2, fin, snd, rcv,
               hk_recv, hv_recv, hsnd, hrcv, ld, xbuf, mbuf, gnm, gmid, ot, hat, wo, dgain):
    rows, toks, width, hd, ff = dims
    ext, total = toks + WINDOW, rows * toks
    pw = 2 * head_dim
    n_pairs = hd // pw
    nb, nc, sub = ff // CB, width // CB, ff // width
    rpd = width // n
    n_mlp, n_down = nb, nc * sub // 2
    per, half_sub = CB // pw, sub // 2
    n_tail = 4 * nc + 1
    pairs = n_mlp + n_down + (n_tail + 1) // 2
    base = n_mlp + n_down
    comm = Torus(n, pairs, n_tail % 2 == 1, parts, recv0, recv1, recv2, recv3, recv4, acc, acc2, fin, snd, rcv)
    me = lax.axis_index("seq")
    right, left = lax.rem(me + 1, n), lax.rem(me + n - 1, n)

    def load(i, s, d):
        c = pltpu.make_async_copy(s, d, ld.at[i])
        c.start()
        return c

    ld_x, ld_m, ld_ot, ld_hat, ld_wo = load(0, dout_h, xbuf), load(1, xm_h, mbuf), load(2, ot_h, ot), load(3, hat_h, hat), load(4, wo_h, wo)
    barrier = pltpu.get_barrier_semaphore()
    peers = comm.peers() + [left, right]
    for other in peers:
        pl.semaphore_signal(barrier, inc=1, device_id={"seq": other}, device_id_type=MESH)
    pl.semaphore_wait(barrier, len(peers))

    def put(idx, value):
        parts[(base + idx // 2) % RING, idx % 2] = value.reshape(n // 2, 2, rpd, CB)

    def mlp(hm, hmt, actt, wgu, wd, dgu, wld):
        def weights(j, slot):
            c = pl.multiple_of(j * CB, CB)
            return [pltpu.make_async_copy(wg_h.at[:, pl.ds(c, CB)], wgu.at[slot, :, pl.ds(0, CB)], wld.at[slot, 0]),
                    pltpu.make_async_copy(wu_h.at[:, pl.ds(c, CB)], wgu.at[slot, :, pl.ds(CB, CB)], wld.at[slot, 1]),
                    pltpu.make_async_copy(wd_h.at[pl.ds(c, CB), :], wd.at[slot], wld.at[slot, 2])]

        for c in weights(0, 0):
            c.start()
        ld_hm, ld_hmt = load(5, hm_h, hm), load(6, hmt_h, hmt)
        gnm[...] = jnp.zeros_like(gnm)
        ld_hm.wait()
        ld_x.wait()
        ld_hmt.wait()

        def block(j):
            slot = j % 2
            for c in weights(j, slot):
                c.wait()

            @pl.when(j + 1 < nb)
            def _():
                for c in weights(j + 1, 1 - slot):
                    c.start()

            c0 = pl.multiple_of(j * CB, CB)
            for b in range(rows):
                r = slice(b * toks, (b + 1) * toks)
                gu = dot(hm[r, :], wgu[slot])
                gact = dot(xbuf[r, :], wd[slot], NT).astype(BF).astype(F32)
                gate, up = gu[:, :CB], gu[:, CB:]
                sig = 1.0 / (1.0 + jnp.exp(-gate))
                swish = gate * sig
                actt[pl.ds(c0, CB), r] = (swish * up).astype(BF).T
                dgu[r, :CB] = (gact * up * (sig + swish * (1.0 - sig))).astype(BF)
                dgu[r, CB:] = (gact * swish).astype(BF)
            both = dot(hmt[...], dgu[...])
            parts[j % RING, 0] = both[:, :CB].reshape(n // 2, 2, rpd, CB)
            parts[j % RING, 1] = both[:, CB:].reshape(n // 2, 2, rpd, CB)
            for b in range(rows):
                r = slice(b * toks, (b + 1) * toks)
                gnm[r, :] += dot(dgu[r, :], wgu[slot], NT)
            comm.tick(j)

        cdiv_loop(nb, block)

        def down(c):
            share = n // 2 // sub
            c0 = pl.multiple_of(c * CB, CB)
            for m in range(sub):
                res = dot(actt[m * width:(m + 1) * width, :], xbuf[:, pl.ds(c0, CB)]).reshape(share, 2, sub, rpd, CB)
                for i in range(sub):
                    pair = n_mlp + c * half_sub + i // 2
                    parts[pair % RING, i % 2, m * share:(m + 1) * share] = res[:, :, i]

        ld_m.wait()
        dgain[...] = jnp.zeros_like(dgain)

        def mid(i):
            r = pl.ds(pl.multiple_of(i * QB, QB), QB)
            out, dg = norm_back(mbuf[r, :], gm[...], gnm[r, :], xbuf[r, :])
            gmid[r, :] = out
            dgain[8:16, :] += dg

        def column(c):
            down(c)
            comm.tick(n_mlp + c * half_sub)

            @pl.when(c == 0)
            def _():
                cdiv_loop(total // QB, mid)

            @pl.when(c < nc - 1)
            def _():
                for e in range(1, half_sub):
                    comm.tick(n_mlp + c * half_sub + e)

        cdiv_loop(nc, column)

    vm = lambda *s: pltpu.VMEM(s, BF)
    pl.run_scoped(mlp, vm(total, width), vm(width, total), vm(ff, total), vm(2, width, 2 * CB), vm(2, CB, width), vm(total, 2 * CB),
                  pltpu.SemaphoreType.DMA((2, 3)))

    def attention(q, kt, k, v, dot_, dqt, dkt, dk, dv, hk, hv, wq, wk, wv):
        lds = [load(5 + i, s, d) for i, (s, d) in enumerate(((q_h, q), (kt_h, kt), (k_h, k), (v_h, v)))]
        ldw = [load(9 + i, s, d) for i, (s, d) in enumerate(((wq_h, wq), (wk_h, wk), (wv_h, wv)))]
        ld_x2 = load(0, x_h, xbuf)
        ld_ot.wait()
        ld_wo.wait()
        dot_[...] = dot(wo[...], gmid[...], NT).astype(BF)
        for e in range(1, half_sub):
            comm.tick(base - half_sub + e)

        def out_grad(g):
            put(g, dot(ot[...], gmid[:, pl.ds(pl.multiple_of(g * CB, CB), CB)]))

        cdiv_loop(nc, out_grad)
        for c in lds:
            c.wait()
        ld_hat.wait()
        upper = upper_mask()
        first = me == 0
        tb = toks // QB

        def attend(p, b):
            r = pl.multiple_of(p * pw, pw)
            ks, vs = [], []
            for blk in range(tb):
                cols = pl.ds(pl.multiple_of(b * toks + blk * QB, QB), QB)
                keys = pl.ds(pl.multiple_of(b * ext + blk * QB, QB), 3 * QB)
                bias0, bias1 = start_bias(first, blk)
                q_stack = stack_pair(q[pl.ds(r, pw), cols])
                do_stack = stack_pair(dot_[pl.ds(r, pw), cols])
                p02, p1 = probs(k[keys, pl.ds(r, pw)], q_stack, upper, bias0, bias1)
                dp = dot(v[keys, pl.ds(r, pw)], do_stack)
                dp02, dp1 = jnp.where(upper, dp[:QB], dp[2 * QB:]), dp[QB:2 * QB]
                mean = jnp.sum(p02 * dp02 + p1 * dp1, axis=0, keepdims=True)
                ds = banded(p02 * (dp02 - mean), p1 * (dp1 - mean), upper)
                vs.append(dot(banded(p02, p1, upper), do_stack, NT))
                ks.append(dot(ds, q_stack, NT))
                dq = unstack_pair(dot(kt[pl.ds(r, pw), keys], ds)) * (head_dim ** -0.5)
                dqt[pl.ds(r, pw), cols] = rope(dq, cos_i[:, cols], sin_i[:, cols], -1, head_dim).astype(BF)
            for parts_, own, halo in ((ks, dk, hk), (vs, dv, hv)):
                for j in range(tb + 2):
                    val = sum(parts_[i][(j - i) * QB:(j - i + 1) * QB] for i in range(tb) if 0 <= j - i < 3).astype(BF)
                    if j < 2:
                        halo[p, b, j * QB:(j + 1) * QB, :] = val
                    else:
                        own[pl.ds(pl.multiple_of(b * toks + (j - 2) * QB, QB), QB), pl.ds(r, pw)] = val

        def halo_copies(p):
            return [pltpu.make_async_remote_copy(src_ref=s.at[p], dst_ref=d.at[p], send_sem=hsnd.at[i, p], recv_sem=hrcv.at[i, p],
                                                 device_id={"seq": left}, device_id_type=MESH)
                    for i, (s, d) in enumerate(((hk, hk_recv), (hv, hv_recv)))]

        def finish(p):
            r = pl.multiple_of(p * pw, pw)
            for c in halo_copies(p):
                c.wait()
            for b in range(rows):
                for blk in range(tb):
                    cols = slice(b * toks + blk * QB, b * toks + (blk + 1) * QB)
                    gk = dk[cols, pl.ds(r, pw)].astype(F32)
                    off = blk * QB - (toks - WINDOW)
                    if off >= 0:
                        gk = gk + hk_recv[p, b, off:off + QB, :].astype(F32)
                        gv = dv[cols, pl.ds(r, pw)].astype(F32) + hv_recv[p, b, off:off + QB, :].astype(F32)
                        dv[cols, pl.ds(r, pw)] = gv.astype(BF)
                    dkt[pl.ds(r, pw), cols] = rope(gk.T, cos_i[:, cols], sin_i[:, cols], -1, head_dim).astype(BF)

        def step(p):
            @pl.when(p < n_pairs)
            def _():
                cdiv_loop(rows, functools.partial(attend, p))
                for c in halo_copies(p):
                    c.start()

            g = p // per

            @pl.when(p % per == per - 1)
            def _():
                put(nc + 3 * g, dot(hat[...], dqt[pl.ds(pl.multiple_of(g * CB, CB), CB), :], NT))

            @pl.when((p % per == 0) & (p > 0))
            def _():
                cdiv_loop(per, lambda i: finish((g - 1) * per + i))
                cols = pl.ds(pl.multiple_of((g - 1) * CB, CB), CB)
                put(nc + 3 * g - 2, dot(hat[...], dkt[cols, :], NT))
                put(nc + 3 * g - 1, dot(hat[...], dv[:, cols]))

            chunks = nc + 3 * (p // per) + (p % per) // (per - 1)

            @pl.when(chunks // 2 > before(p) // 2)
            def _():
                comm.tick(base + chunks // 2 - 1)

        def before(p):
            return jnp.where(p == 0, nc // 2 * 2 - 2, nc + 3 * ((p - 1) // per) + ((p - 1) % per) // (per - 1))

        cdiv_loop(n_pairs + 1, step)
        for c in ldw:
            c.wait()
        ld_x2.wait()

        def into(b):
            r = pl.ds(pl.multiple_of(b * toks, QB), toks)
            gnm[r, :] = dot(dqt[:, r], wq[...], TN) + dot(dkt[:, r], wk[...], TN) + dot(dv[r, :], wv[...])

        def final(i):
            r = pl.ds(pl.multiple_of(i * QB, QB), QB)
            out, dg = norm_back(xbuf[r, :], ga[...], gnm[r, :], gmid[r, :])
            mbuf[r, :] = out
            dgain[0:8, :] += dg

        cdiv_loop(rows, into)
        cdiv_loop(total // QB, final)

    pl.run_scoped(attention, vm(hd, total), vm(hd, rows * ext), vm(rows * ext, hd), vm(rows * ext, hd), vm(hd, total), vm(hd, total), vm(hd, total),
                  vm(total, hd), vm(total, hd), vm(n_pairs, rows, WINDOW, pw), vm(n_pairs, rows, WINDOW, pw), vm(hd, width), vm(hd, width), vm(hd, width))
    out_copy = load(1, mbuf, dx_h)
    wide = jnp.concatenate([dgain[...], jnp.zeros((CB - dgain.shape[0], width), F32)], axis=0)
    put(n_tail - 1, wide.T)
    lax.fori_loop(pairs - 1, pairs + 5 * LAG, lambda t, c: (comm.tick(t), c)[1], 0)

    for j in range(nb):
        dg_o[:, j * CB:(j + 1) * CB] = fin[2 * j]
        du_o[:, j * CB:(j + 1) * CB] = fin[2 * j + 1]
    for c in range(nc):
        cols = slice(c * CB, (c + 1) * CB)
        for i in range(sub):
            dd_o[i * rpd:(i + 1) * rpd, cols] = fin[2 * n_mlp + c * sub + i]
    for g in range(nc):
        do_o[:, g * CB:(g + 1) * CB] = fin[2 * base + g]
        for i, ref in enumerate((dq_o, dk_o, dv_o)):
            val = fin[2 * base + nc + 3 * g + i]
            for h in range(CB // head_dim):
                ref[g * (CB // head_dim) + h] = val[:, h * head_dim:(h + 1) * head_dim]
    sums = fin[2 * base + n_tail - 1][:, :128].T
    dga_o[...] = jnp.sum(sums[0:8], axis=0, keepdims=True)
    dgm_o[...] = jnp.sum(sums[8:16], axis=0, keepdims=True)
    out_copy.wait()


def run_bwd(n, head_dim, ga, gm, x, dout, q, kt, k, v, hat, ot, xm, hm, hmt, cos_t, sin_t, wq, wk, wv, wo, wg, wu, wd, rows):
    total, width = x.shape
    hd, ff = wq.shape[0], wg.shape[1]
    toks = total // rows
    rpd, heads = width // n, hd // head_dim
    nb, nc, sub = ff // CB, width // CB, ff // width
    pairs = nb + nc * sub // 2 + (4 * nc + 2) // 2
    n_pairs = hd // (2 * head_dim)
    f = lambda *s: jax.ShapeDtypeStruct(s, F32)
    outs = [jax.ShapeDtypeStruct((total, width), BF), f(1, rpd), f(1, rpd)] + [f(heads, rpd, head_dim)] * 3 + [f(rpd, width), f(rpd, ff), f(rpd, ff), f(ff // n, width)]
    vm = lambda *s: pltpu.VMEM(s, BF)
    vf = lambda *s: pltpu.VMEM(s, F32)
    dma = lambda *s: pltpu.SemaphoreType.DMA(s)
    scratch = [vf(RING, 2, n // 2, 2, rpd, CB), vf(2, SLOTS, n // 2, rpd, CB), vf(2, SLOTS, 2, 2, rpd, CB), vf(2, SLOTS, 2, 4, rpd, CB),
               vf(2, SLOTS, 2, rpd, CB // 2), vf(2, SLOTS, 2, rpd, CB), vf(2, SLOTS, 4, 4, rpd, CB), vf(2, SLOTS, 4, rpd, CB), vf(2 * pairs, rpd, CB),
               dma(9, 2, SLOTS), dma(9, 2, SLOTS),
               vm(n_pairs, rows, WINDOW, 2 * head_dim), vm(n_pairs, rows, WINDOW, 2 * head_dim), dma(2, n_pairs), dma(2, n_pairs), dma(12),
               vm(total, width), vm(total, width), vf(total, width), vm(total, width), vm(hd, total), vm(width, total), vm(hd, width), vf(16, width)]
    return pl.pallas_call(
        functools.partial(bwd_kernel, n, head_dim, (rows, toks, width, hd, ff)), out_shape=outs,
        in_specs=vmem_spec(2) + any_spec(11) + vmem_spec(2) + any_spec(7), out_specs=any_spec(1) + vmem_spec(9), scratch_shapes=scratch,
        compiler_params=pltpu.CompilerParams(collective_id=1, has_side_effects=True, vmem_limit_bytes=VMEM_LIMIT),
        name="backward")(ga, gm, x, dout, q, kt, k, v, hat, ot, xm, hm, hmt, cos_t, sin_t, wq, wk, wv, wo, wg, wu, wd)


def solution(mesh):
    n = mesh.shape["seq"]

    def device_step(hidden, positions, g_attn, g_mlp, w_query, w_key, w_value, w_out, w_gate, w_up, w_down, d_out):
        rows, toks, width = hidden.shape
        layers, _, heads, head_dim = w_query.shape
        hd = heads * head_dim
        half = head_dim // 2
        inv_freq = 1.0 / (10000.0 ** (jnp.arange(half, dtype=F32) * (2.0 / head_dim)))
        turn = lambda w: w[0].transpose(1, 2, 0).reshape(hd, width)
        wq, wk, wv = turn(w_query), turn(w_key), turn(w_value)
        fwd = run_fwd(n, hidden, positions, inv_freq[:, None], g_attn, g_mlp, wq, wk, wv, w_out[0], head_dim)
        out = run_bwd(n, head_dim, g_attn, g_mlp, hidden.reshape(rows * toks, width), d_out.reshape(rows * toks, width), *fwd,
                      wq, wk, wv, w_out[0], w_gate[0], w_up[0], w_down[0], rows)
        dx, dga, dgm, dq, dk, dv, do, dg, du, dd = out
        back = lambda w: w.transpose(1, 0, 2)[None]
        return (dx.reshape(rows, toks, width), dga, dgm, back(dq), back(dk), back(dv), do[None], dg[None], du[None], dd[None])

    tok_spec = P("data", "seq", None)
    vec_spec = P(None, ("data", "seq"))
    mat_spec = P(None, ("data", "seq"), None)
    head_spec = P(None, ("data", "seq"), None, None)
    in_specs = (tok_spec, P("data", "seq")) + (P(),) * 9 + (tok_spec,)
    out_specs = (tok_spec, vec_spec, vec_spec, head_spec, head_spec, head_spec, mat_spec, mat_spec, mat_spec, mat_spec)
    return jax.shard_map(device_step, mesh=mesh, in_specs=in_specs, out_specs=out_specs, check_vma=False)
```

time: 937 us -> 236 us (0.25)
  waiting for transfers between devices: 403 us -> 0 us
  matrix products: 251 us -> 0 us
  Pallas kernels: 0 us -> 225 us
  local copies, waits for them, and re-layouts: 150 us -> 8.7 us
  blocking collectives: 51.3 us -> 0 us
  other arithmetic: 41.4 us -> 0.62 us
  between operations: 15.1 us -> 0.73 us
  starting transfers between devices: 11.2 us -> 0 us
    reduce_scatter x7 -> x0, waiting for transfers between devices: 370 us -> none  [scatter_sum(): return lax.psum_scatter(partial_sum, 'seq', scatter_dimension=0, tiled=True)]
    dot_general x41 -> x0, matrix products: 251 us -> none  [the longest x12 64.8 us: one_block(): jnp.einsum('bqkgd,bckd->bkgqc', q_blk, k_blk, preferred_element_type=jnp....]
    pallas_call x0 -> x2, Pallas kernels: none -> 225 us  [the longest x1 173 us: run_bwd(): pl.pallas_call(functools.partial(bwd_kernel, n, head_dim, (rows, toks, wi...]
    add_any x6 -> x0, local copies, waits for them, and re-layouts: 86.6 us -> none  [window_attention(): blocks = lax.map(jax.checkpoint(one_block), jnp.arange(tok_local // qblock))]
    unnamed x1 -> x0, blocking collectives: 51.3 us -> none
    ppermute x4 -> x0, waiting for transfers between devices: 32.7 us -> none  [the longest x1 14.3 us: device_step(): v_back = lax.ppermute(grad_v_ext[:, :halo_len], 'seq', to_left)]
    reduce_sum x7 -> x0, other arithmetic: 13.8 us -> none  [the longest x6 11.9 us: one_block(): jax.nn.softmax(jnp.where(keep_mask, scores, -1e+30), axis=-1)]
    while x54 -> x0, local copies, waits for them, and re-layouts: 12.4 us -> none
  transfers between devices with their start and end apart: 11 -> 0, of which waited for: 8 -> 0; matrix products, arithmetic and copies ran while one was open for 32% -> 0% of each run, Pallas kernels for 0% -> 0%
where the time goes in v1:
time: 236 us; the launch traced here: 235 us
  Pallas kernels  225 us (95%)
  local copies, waits for them, and re-layouts  8.7 us (4%)
    pallas_call x1, Pallas kernels, run_bwd(): pl.pallas_call(functools.partial(bwd_kernel, n, head_dim, (rows, toks, wi...  173 us
    pallas_call x1, Pallas kernels, run_fwd(): pl.pallas_call(functools.partial(fwd_kernel, n, head_dim), out_shape=outs...  51.6 us
    unnamed x28, local copies, waits for them, and re-layouts  8.7 us

profile of v1, /device:TPU:97, one launch (start us, length us, event | category | flops | bytes accessed | tf_op | source)
XLA Modules:
  0.0 235.0 jit_solution(9937309238087863633)
XLA Ops:
  0.6 0.6 negate_power_fusion.invf
  1.3 51.6 %forward.1 = (bf16[768,1152]{1,0:T(8,128)(2,1)}, bf16[768,1920]{1,0:T(8,128)(2,1)}, bf16[1920,768]{1,0:T(8,128)(2,1)}, bf16[1920,768]{1,0:T(8,128)(2,1)}, bf16[7...) custom-call(bf16[3,384,768]{2,1,0:T(8,128)(2,1)} %x_h.1, ...), custom_call_target="tpu_custom_call" | custom-call | tf_op jit(solution)/shard_map/forward/pallas_call | solution.py:241
  52.9 173.3 %backward.1 = (bf16[1152,768]{1,0:T(8,128)(2,1)}, f32[1,24]{1,0:T(1,128)}, f32[1,24]{1,0:T(1,128)}, f32[12,24,64]{2,1,0:T(8,128)}, f32[12,24,64]{2,1,0:T(8,128)}...) custom-call(f32[1,768]{1,0:T(1,128)} %ga.3, ...), custom_call_target="tpu_custom_call" | custom-call | tf_op jit(solution)/shard_map/backward/pallas_call | solution.py:641
  226.2 0.0 copy-start.8
  226.2 0.0 copy-start.7
  226.2 0.0 copy-start.5
  226.2 0.0 copy-start.4
  226.2 0.0 copy-start.3
  226.2 0.0 copy-start.6
  226.3 0.0 copy-start.2
  226.3 0.0 copy-start.1
  226.3 2.9 %copy.32 = bf16[3,384,768]{2,1,0:T(8,128)(2,1)} copy(bf16[3,384,768]{2,1,0:T(8,128)(2,1)} %bitcast.47) | data formatting | bytes 3538944
  229.2 0.0 copy-done.8
  229.2 0.0 copy-start
  229.2 0.5 copy.33
  229.7 0.0 copy-done.7
  229.7 0.5 copy.34
  230.2 0.0 copy-done.5
  230.2 0.7 copy.35
  230.8 0.0 copy-done.4
  230.9 0.7 copy.36
  231.5 0.0 copy-done.3
  231.5 0.7 copy.37
  232.2 0.0 copy-done.6
  232.2 0.6 copy.38
  232.8 0.0 copy-done.2
  232.8 0.7 copy.39
  233.5 0.0 copy-done.1
  233.5 0.7 copy.40
  234.2 0.0 copy-done
  234.2 0.7 copy.41
Async XLA Ops:
  226.2 3.0 %copy-start.8 = (f32[1,24]{1,0:T(1,128)S(1)}, f32[1,24]{1,0:T(1,128)}, u32[]{:S(2)}) copy-start(f32[1,24]{1,0:T(1,128)} %get-tuple-element.63) | copy-start | bytes 292
  226.2 3.5 %copy-start.7 = (f32[1,24]{1,0:T(1,128)S(1)}, f32[1,24]{1,0:T(1,128)}, u32[]{:S(2)}) copy-start(f32[1,24]{1,0:T(1,128)} %get-tuple-element.64) | copy-start | bytes 292
  226.2 4.0 %copy-start.5 = (f32[12,24,64]{2,1,0:T(8,128)S(1)}, f32[12,24,64]{2,1,0:T(8,128)}, u32[]{:S(2)}) copy-start(f32[12,24,64]{2,1,0:T(8,128)} %get-tuple-element.45) | copy-start | bytes 221188
  226.2 4.6 %copy-start.4 = (f32[12,24,64]{2,1,0:T(8,128)S(1)}, f32[12,24,64]{2,1,0:T(8,128)}, u32[]{:S(2)}) copy-start(f32[12,24,64]{2,1,0:T(8,128)} %get-tuple-element.46) | copy-start | bytes 221188
  226.2 5.3 %copy-start.3 = (f32[12,24,64]{2,1,0:T(8,128)S(1)}, f32[12,24,64]{2,1,0:T(8,128)}, u32[]{:S(2)}) copy-start(f32[12,24,64]{2,1,0:T(8,128)} %get-tuple-element.47) | copy-start | bytes 221188
  226.2 5.9 %copy-start.6 = (f32[24,768]{1,0:T(8,128)S(1)}, f32[24,768]{1,0:T(8,128)}, u32[]{:S(2)}) copy-start(f32[24,768]{1,0:T(8,128)} %get-tuple-element.48) | copy-start | bytes 221188
  226.3 6.6 %copy-start.2 = (f32[24,3072]{1,0:T(8,128)S(1)}, f32[24,3072]{1,0:T(8,128)}, u32[]{:S(2)}) copy-start(f32[24,3072]{1,0:T(8,128)} %get-tuple-element.49) | copy-start | bytes 884740
  226.3 7.3 %copy-start.1 = (f32[24,3072]{1,0:T(8,128)S(1)}, f32[24,3072]{1,0:T(8,128)}, u32[]{:S(2)}) copy-start(f32[24,3072]{1,0:T(8,128)} %get-tuple-element.50) | copy-start | bytes 884740
  229.2 5.1 %copy-start = (f32[96,768]{1,0:T(8,128)S(1)}, f32[96,768]{1,0:T(8,128)}, u32[]{:S(2)}) copy-start(f32[96,768]{1,0:T(8,128)} %get-tuple-element.51) | copy-start | bytes 884740
